TPU v7x, 512 devices: a whole 4x4x16 slice. The times are simulated.
512 devices in a mesh: grp: 8 (over x, z_hi), seq: 64 (over y, z_lo, core).
Axes of the slice: x: 4, y: 4, z: 16 (z_hi: 2, z_lo: 8; z = z_hi * 8 + z_lo), core: 2. Of those that a mesh axis runs over, the one named last changes fastest.
Arguments:
- queries: bfloat16 [512, 5120], P(('grp', 'seq')), may hold values from -10 to 10
- query_tangent: bfloat16 [512, 5120], P(('grp', 'seq')), may hold values from -6 to 6
- keys: bfloat16 [32768, 5120], P('seq', 'grp'), may hold values from -10 to 10
- key_tangent: bfloat16 [32768, 5120], P('seq', 'grp'), may hold values from -6 to 6
- values: bfloat16 [32768, 5120], P('seq', 'grp'), may hold values from -6 to 6
- value_tangent: bfloat16 [32768, 5120], P('seq', 'grp'), may hold values from -6 to 6
Outputs:
- attended: bfloat16 [512, 5120], P(('grp', 'seq'))
- attended_tangent: bfloat16 [512, 5120], P(('grp', 'seq'))
All inputs are finite; a program needn't handle non-finite values.
Results may differ from a plain program's by a relative error of at most 0.0084.
Values may be sent and summed in bfloat16 or wider, within the bound.
A program may use at most 64 MiB of HBM per device.

v0:
```python
import jax
import jax.numpy as jnp
from jax import lax
from jax.sharding import PartitionSpec as P

HEAD_DIM = 128


def split_up(shard, dim, peers):
    lengths = shard.shape
    parts = shard.reshape(*lengths[:dim], peers, lengths[dim] // peers, *lengths[dim + 1 :])
    return jnp.moveaxis(parts, dim, 0)


def piece_ends(length, count):
    unit = 8 if length >= 8 * count else 1
    return [length // unit * k // count * unit for k in range(1, count)]


def in_order(parts, dim):
    parts = jnp.moveaxis(parts, 0, dim)
    lengths = parts.shape
    return parts.reshape(*lengths[:dim], lengths[dim] * lengths[dim + 1], *lengths[dim + 2 :])


def several_exchanges(shard, axis, pieces, split_dim, concat_dim):
    parts = split_up(shard, split_dim, lax.axis_size(axis))
    widest = max(range(1, max(2, parts.ndim - 1)), key=lambda d: parts.shape[d])
    gathered = []
    for slab in jnp.split(parts, piece_ends(parts.shape[widest], pieces), axis=widest):
        if slab.size:
            gathered.append(lax.all_to_all(slab, axis, split_axis=0, concat_axis=0, tiled=True))
    return in_order(jnp.concatenate(gathered, axis=widest), concat_dim)


def side_by_side(arrays, axis, dim, along):
    both = jnp.concatenate(arrays, axis=along)
    result, at, gathered = (lax.all_gather(both, axis, axis=dim, tiled=True), 0, [])
    for a in arrays:
        gathered.append(lax.slice_in_dim(result, at, at + a.shape[along], axis=along))
        at += a.shape[along]
    return tuple(gathered)


def sent_together(arrays, axis, split_dim, concat_dim, along):
    both = jnp.concatenate(arrays, axis=along)
    result, at, gathered = (
        lax.all_to_all(both, axis, split_axis=split_dim, concat_axis=concat_dim, tiled=True),
        0,
        [],
    )
    for a in arrays:
        gathered.append(lax.slice_in_dim(result, at, at + a.shape[along], axis=along))
        at += a.shape[along]
    return tuple(gathered)


def per_device(queries, query_tangent, keys, key_tangent, values, value_tangent):
    n_seq = lax.axis_size("seq")
    width = keys.shape[1]
    head_count = width // HEAD_DIM
    key_count = keys.shape[0]
    local_heads = (
        several_exchanges(queries, "grp", 2, 1, 0),
        several_exchanges(query_tangent, "grp", 2, 1, 0),
    )
    slab_query, slab_tangent = side_by_side((local_heads[0], local_heads[1]), "seq", 0, 1)
    rows = slab_query.shape[0]
    query3 = slab_query.reshape(rows, head_count, HEAD_DIM)
    qtan3 = slab_tangent.reshape(rows, head_count, HEAD_DIM)
    key3 = keys.reshape(key_count, head_count, HEAD_DIM)
    ktan3 = key_tangent.reshape(key_count, head_count, HEAD_DIM)
    value3 = values.reshape(key_count, head_count, HEAD_DIM)
    vtan3 = value_tangent.reshape(key_count, head_count, HEAD_DIM)
    scale = HEAD_DIM ** (-0.5)
    logit_scores = (
        jnp.einsum("qhd,khd->hqk", query3, key3, preferred_element_type=jnp.float32) * scale
    )
    tangent_scores = (
        jnp.einsum("qhd,khd->hqk", qtan3, key3, preferred_element_type=jnp.float32)
        + jnp.einsum("qhd,khd->hqk", query3, ktan3, preferred_element_type=jnp.float32)
    ) * scale
    local_max = jnp.max(logit_scores, axis=2)
    weights = jnp.exp(logit_scores - local_max[:, :, None])
    mixed = weights * tangent_scores
    total = jnp.sum(weights, axis=2).T
    total_tangent = jnp.sum(mixed, axis=2).T
    weights_reduced_precision = weights.astype(jnp.bfloat16)
    mixed_reduced_precision = mixed.astype(jnp.bfloat16)
    numer = jnp.einsum(
        "hqk,khd->qhd", weights_reduced_precision, value3, preferred_element_type=jnp.float32
    )
    numer_tangent = jnp.einsum(
        "hqk,khd->qhd", weights_reduced_precision, vtan3, preferred_element_type=jnp.float32
    ) + jnp.einsum(
        "hqk,khd->qhd", mixed_reduced_precision, value3, preferred_element_type=jnp.float32
    )
    sent = (
        numer.reshape(1, rows, width),
        numer_tangent.reshape(1, rows, width),
        total[None],
        total_tangent[None],
        local_max.T[None],
    )
    got_numer, got_tangent, got_total, got_dtotal, got_max = sent_together(
        (sent[0], sent[1], sent[2], sent[3], sent[4]), "seq", 1, 0, 2
    )
    share = got_max.shape[1]
    whole_max = jnp.max(got_max, axis=0)
    factor = jnp.exp(got_max - whole_max[None])
    own_numer = jnp.sum(
        got_numer.reshape(n_seq, share, head_count, HEAD_DIM) * factor[:, :, :, None], axis=0
    ).reshape(share, width)
    own_tangent = jnp.sum(
        got_tangent.reshape(n_seq, share, head_count, HEAD_DIM) * factor[:, :, :, None], axis=0
    ).reshape(share, width)
    own_total = jnp.sum(got_total * factor, axis=0)
    own_dtotal = jnp.sum(got_dtotal * factor, axis=0)
    owned = own_numer.shape[0]
    output = own_numer.reshape(owned, head_count, HEAD_DIM) / own_total[:, :, None]
    out_tangent = (
        own_tangent.reshape(owned, head_count, HEAD_DIM) - output * own_dtotal[:, :, None]
    ) / own_total[:, :, None]
    output_low = output.reshape(owned, width).astype(jnp.bfloat16)
    tangent_low = out_tangent.reshape(owned, width).astype(jnp.bfloat16)
    attended, attended_tangent = (
        lax.all_to_all(output_low, "grp", split_axis=0, concat_axis=1, tiled=True),
        lax.all_to_all(tangent_low, "grp", split_axis=0, concat_axis=1, tiled=True),
    )
    return (attended, attended_tangent)


def solution(mesh):
    in_specs = (
        P(("grp", "seq"), None),
        P(("grp", "seq"), None),
        P("seq", "grp"),
        P("seq", "grp"),
        P("seq", "grp"),
        P("seq", "grp"),
    )
    out_specs = (P(("grp", "seq"), None), P(("grp", "seq"), None))
    return jax.shard_map(
        per_device, mesh=mesh, in_specs=in_specs, out_specs=out_specs, check_vma=False
    )
```

profile of v0, /device:TPU:1, one launch (start us, length us, event | category | flops | bytes accessed | tf_op | source)
XLA Modules:
  0.0 400.4 jit_solution(12298076516029851253)
XLA Ops:
  7.7 1.5 reduce.2
  9.9 18.1 %all-to-all-start.1 = ((bf16[8,2,320]{2,1,0:T(2,128)(2,1)}), bf16[8,2,320]{2,1,0:T(2,128)(2,1)S(1)}, u32[]{:S(2)}, u32[]{:S(2)}) async-start(bf16[8,2,320]{2,1,0:T(2,128)(2,1)} %reshape.137), calls=%async_computation.1 | async-start | bytes 24576 | tf_op jit(solution)/shard_map/all_to_all | solution.py:32
  28.0 1.5 reduce.3
  30.1 11.6 %all-to-all-done.1 = bf16[8,2,320]{2,1,0:T(2,128)(2,1)S(1)} async-done(((bf16[8,2,320]{2,1,0:T(2,128)(2,1)}), bf16[8,2,320]{2,1,0:T(2,128)(2,1)S(1)}, u32[]{:S(2)}, u32[]{:S(2)}) %all-to-all-start.1) | async-done | bytes 10272 | tf_op jit(solution)/shard_map/all_to_all | solution.py:32
  41.7 3.3 all-to-all-start
  45.3 13.5 %all-to-all-done = bf16[8,2,320]{2,1,0:T(2,128)(2,1)S(1)} async-done(((bf16[8,2,320]{2,1,0:T(2,128)(2,1)}), bf16[8,2,320]{2,1,0:T(2,128)(2,1)S(1)}, u32[]{:S(2)}, u32[]{:S(2)}) %all-to-all-start) | async-done | bytes 10272 | tf_op jit(solution)/shard_map/all_to_all | solution.py:32
  59.5 1.3 copy.133
  60.9 1.3 copy.143
  62.2 1.3 copy.138
  63.5 1.3 copy.136
  64.9 110.8 %all-gather.2.cloned.1.call-done = bf16[512,1280]{1,0:T(8,128)(2,1)} async-done(((bf16[8,1280]{1,0:T(8,128)(2,1)}), bf16[512,1280]{1,0:T(8,128)(2,1)}) %all-gather.2.cloned.1.call-update) | async-done | bytes 1310736 | tf_op jit(solution)/shard_map/all_gather | solution.py:38
  175.7 2.5 fusion.20
  178.2 1.3 copy.169
  179.5 2.2 copy.170
  181.7 0.9 multiply_reduce_fusion
  182.8 0.9 fusion.22
  183.6 0.9 fusion
  184.5 1.1 fusion.11
  185.6 1.1 fusion.9
  186.7 1.9 fusion.21
  188.7 1.6 fusion.4
  190.3 3.7 copy.148
  194.2 2.1 copy.147
  196.5 0.9 copy.151
  197.3 15.1 %concatenate.7 = f32[1,512,1295]{2,0,1:T(1,128)S(1)} concatenate(f32[1,512,640]{2,0,1:T(1,128)} %copy.147, f32[1,512,640]{2,0,1:T(1,128)} %copy.148, f32[1,512,5]{2,0,1:T(1,128)S(1)} %copy.149, f32[1,512,5]{2,0,1:T(1,128)S(1)} %copy.150, f32[1,512,5]{2,0,1:T(1,128)} %copy.151), dimensions={2} | concatenate | bytes 5304320 | tf_op jit(solution)/shard_map/concatenate | solution.py:46
  212.4 136.6 %all_to_all.48 = f32[1,512,1295]{2,0,1:T(1,128)S(1)} all-to-all(f32[1,512,1295]{2,0,1:T(1,128)S(1)} %concatenate.7), channel_id=1, replica_groups=mesh['grp'=8,'seq'=64] {'seq'}, dimensions={1} | all-to-all | bytes 5304320 | tf_op jit(solution)/shard_map/all_to_all | solution.py:48
  352.1 9.9 %all-to-all-start.4 = ((bf16[8,2,320]{2,1,0:T(2,128)(2,1)}), bf16[8,2,320]{2,1,0:T(2,128)(2,1)S(1)}, u32[]{:S(2)}, u32[]{:S(2)}) async-start(bf16[8,2,320]{2,1,0:T(2,128)(2,1)} %reshape.143), calls=%async_computation.4 | async-start | bytes 24576 | tf_op jit(solution)/shard_map/all_to_all | solution.py:128
  363.4 12.4 %all-to-all-done.4 = bf16[8,2,320]{2,1,0:T(2,128)(2,1)S(1)} async-done(((bf16[8,2,320]{2,1,0:T(2,128)(2,1)}), bf16[8,2,320]{2,1,0:T(2,128)(2,1)S(1)}, u32[]{:S(2)}, u32[]{:S(2)}) %all-to-all-start.4) | async-done | bytes 10272 | tf_op jit(solution)/shard_map/all_to_all | solution.py:128
  375.8 3.3 all-to-all-start.3
  379.1 0.7 reshape.144
  379.8 13.0 %all-to-all-done.3 = bf16[8,2,320]{2,1,0:T(2,128)(2,1)S(1)} async-done(((bf16[8,2,320]{2,1,0:T(2,128)(2,1)}), bf16[8,2,320]{2,1,0:T(2,128)(2,1)S(1)}, u32[]{:S(2)}, u32[]{:S(2)}) %all-to-all-start.3) | async-done | bytes 10272 | tf_op jit(solution)/shard_map/all_to_all | solution.py:127
  392.8 0.7 reshape.142
  (26 shorter events, 7.7 us)
Async XLA Ops:
  9.9 31.9 %all-to-all-start.1 = ((bf16[8,2,320]{2,1,0:T(2,128)(2,1)}), bf16[8,2,320]{2,1,0:T(2,128)(2,1)S(1)}, u32[]{:S(2)}, u32[]{:S(2)}) async-start(bf16[8,2,320]{2,1,0:T(2,128)(2,1)} %reshape.137), calls=%async_computation.1 | async-start | bytes 24576 | tf_op jit(solution)/shard_map/all_to_all | solution.py:32
  41.7 17.0 %all-to-all-start = ((bf16[8,2,320]{2,1,0:T(2,128)(2,1)}), bf16[8,2,320]{2,1,0:T(2,128)(2,1)S(1)}, u32[]{:S(2)}, u32[]{:S(2)}) async-start(bf16[8,2,320]{2,1,0:T(2,128)(2,1)} %reshape.139), calls=%async_computation | async-start | bytes 24576 | tf_op jit(solution)/shard_map/all_to_all | solution.py:32
  45.1 130.6 %all-gather.2.cloned.1.call-start = ((), (), s32[]{:S(2)}) async-start(), calls=%async_computation.5 | async-start | bytes 1331200 | tf_op jit(solution)/shard_map/all_gather | solution.py:38
  181.7 1.1 copy-start
  352.1 23.7 %all-to-all-start.4 = ((bf16[8,2,320]{2,1,0:T(2,128)(2,1)}), bf16[8,2,320]{2,1,0:T(2,128)(2,1)S(1)}, u32[]{:S(2)}, u32[]{:S(2)}) async-start(bf16[8,2,320]{2,1,0:T(2,128)(2,1)} %reshape.143), calls=%async_computation.4 | async-start | bytes 24576 | tf_op jit(solution)/shard_map/all_to_all | solution.py:128
  375.8 17.0 %all-to-all-start.3 = ((bf16[8,2,320]{2,1,0:T(2,128)(2,1)}), bf16[8,2,320]{2,1,0:T(2,128)(2,1)S(1)}, u32[]{:S(2)}, u32[]{:S(2)}) async-start(bf16[8,2,320]{2,1,0:T(2,128)(2,1)} %reshape.141), calls=%async_computation.3 | async-start | bytes 24576 | tf_op jit(solution)/shard_map/all_to_all | solution.py:127
Sparse Core Ops, SparseCore 0:
  59.6 115.9 all-gather.1
where the time goes:
time: 404 us; the launch traced here: 400 us
  waiting for transfers between devices  161 us (40%)
  blocking collectives  137 us (34%)
  local copies, waits for them, and re-layouts  39.3 us (10%)
  starting transfers between devices  34.7 us (9%)
  between operations  14.2 us (4%)
  matrix products  7.54 us (2%)
  other arithmetic  6.58 us (2%)
    all_to_all x1, blocking collectives, sent_together(): lax.all_to_all(both, axis, split_axis=split_dim, concat_axis=concat_dim,...  137 us
    all_gather x1, waiting for transfers between devices, side_by_side(): lax.all_gather(both, axis, axis=dim, tiled=True)  111 us
    all_to_all x2, waiting for transfers between devices, several_exchanges(): lax.all_to_all(slab, axis, split_axis=0, concat_axis=0, tiled=True)  25.2 us
    all_to_all x2, starting transfers between devices, several_exchanges(): lax.all_to_all(slab, axis, split_axis=0, concat_axis=0, tiled=True)  21.4 us
    concatenate x1, local copies, waits for them, and re-layouts, sent_together(): both = jnp.concatenate(arrays, axis=along)  15.1 us
    unnamed x19, local copies, waits for them, and re-layouts  13.6 us
    all_to_all x1, waiting for transfers between devices, per_device(): lax.all_to_all(output_low, 'grp', split_axis=0, concat_axis=1, tiled=True)  13 us
    all_to_all x1, waiting for transfers between devices, per_device(): lax.all_to_all(tangent_low, 'grp', split_axis=0, concat_axis=1, tiled=True)  12.4 us
  transfers between devices with their start and end apart: 5, of which 5 were waited for; matrix products, arithmetic and copies ran while one was open for 2% of the time, Pallas kernels for 0%

commit v1 on v0

v1 whole, which is shorter than its diff:
```python
import functools

import jax
import jax.numpy as jnp
from jax import lax
from jax.experimental import pallas as pl
from jax.experimental.pallas import tpu as pltpu
from jax.sharding import PartitionSpec as P

HEAD_DIM = 128
X, Y, ZH, ZL = 4, 4, 2, 8
Z = ZH * ZL
GRP = X * ZH
B = 2 * X
MESH = pl.DeviceIdType.MESH
F32, BF16 = jnp.float32, jnp.bfloat16


def merge(planes, heads):
    count = planes.count
    stats = [planes(i, 2 * heads) for i in range(count)]
    axis = stats[0].ndim - 1
    stats = [s + pltpu.roll(s, 128 - 2 * heads, axis) + pltpu.roll(s, 128 - 4 * heads, axis) for s in stats]
    top = functools.reduce(jnp.maximum, stats)
    grown = [jnp.exp(s - top) for s in stats]
    whole = sum(grown)
    weights = [g / whole for g in grown]
    moved = [pltpu.roll(w, heads, axis) for w in weights]
    score = sum(w * s for w, s in zip(moved, stats))
    tilts = [w * (s - score) for w, s in zip(moved, stats)]
    lane = lax.broadcasted_iota(jnp.int32, top.shape, axis)
    merged = jnp.where(lane < heads, top + jnp.log(whole), score)
    outs, tans = [], []
    for h in range(heads):
        out = tan = None
        for i in range(count):
            w = weights[i][..., h : h + 1]
            c = tilts[i][..., heads + h : heads + h + 1]
            o, t = planes(i, h), planes(i, heads + h)
            a, b = w * o, w * t + c * o
            out, tan = (a, b) if i == 0 else (out + a, tan + b)
        outs.append(out)
        tans.append(tan)
    return outs, tans, merged


def pieces(stats, heads):
    axis = stats.ndim - 1
    lane = lax.broadcasted_iota(jnp.int32, stats.shape, axis)
    stats = jnp.where(lane < 2 * heads, stats, 0.0)
    high = stats.astype(BF16).astype(F32)
    rest = stats - high
    middle = rest.astype(BF16).astype(F32)
    low = (rest - middle).astype(BF16).astype(F32)
    return high + pltpu.roll(middle, 2 * heads, axis) + pltpu.roll(low, 4 * heads, axis)


class Planes:
    def __init__(self, refs):
        self.refs, self.count = refs, len(refs)

    def __call__(self, i, p):
        return self.refs[i][p].astype(F32)


def kernel(heads, q_in, t_in, k_hbm, kt_hbm, v_hbm, vt_hbm, o_out, t_out,
           kk, vv, stage, xrecv, zsend, qbuf, stat, mine, theirs, pair, yrecv, total, zrecv, final, orecv,
           load_sem, xs_sem, xr_sem, zs_sem, zr_sem, fs_sem, fr_sem, ys_sem, yr_sem,
           ps_sem, pr_sem, rs_sem, rr_sem, cs_sem, cr_sem, es_sem, er_sem):
    grp, seq = lax.axis_index("grp"), lax.axis_index("seq")
    x, zh = lax.div(grp, ZH), lax.rem(grp, ZH)
    y, zl, core = lax.div(seq, 2 * ZL), lax.rem(lax.div(seq, 2), ZL), lax.rem(seq, 2)
    z = zh * ZL + zl
    other = 1 - core

    def device(x_, y_, z_, core_):
        return (x_ * ZH + lax.div(z_, ZL), (y_ * ZL + lax.rem(z_, ZL)) * 2 + core_)

    def remote(src, dst, send, recv, where):
        return pltpu.make_async_remote_copy(src_ref=src, dst_ref=dst, send_sem=send, recv_sem=recv,
                                            device_id=where, device_id_type=MESH)

    here = (grp, seq)
    partner = (grp, seq + 1 - 2 * core)
    planes = 2 * heads + 1

    barrier = pltpu.get_barrier_semaphore()

    def greet(where):
        pl.semaphore_signal(barrier, inc=1, device_id=where, device_id_type=MESH)

    for k in range(1, Z):
        greet(device(x, y, lax.rem(z + k, Z), core))

    @pl.when(core != zh)
    def _():
        for i in range(ZL):
            greet(device(x, y, core * ZL + i, zh))

    for d in range(1, Y):
        greet(device(x, lax.rem(y + d, Y), z, core))
    for d in range(X):
        if d:
            greet(device(lax.rem(x + d, X), y, z, core))
        greet(device(lax.rem(x + d, X), y, z, other))

    loads = []
    for h in range(heads):
        cols = pl.ds(h * HEAD_DIM, HEAD_DIM)
        loads += [
            pltpu.make_async_copy(k_hbm.at[:, cols], kk.at[h, :, pl.ds(0, HEAD_DIM)], load_sem.at[h, 0]),
            pltpu.make_async_copy(kt_hbm.at[:, cols], kk.at[h, :, pl.ds(HEAD_DIM, HEAD_DIM)], load_sem.at[h, 1]),
            pltpu.make_async_copy(v_hbm.at[:, cols], vv.at[h, :, pl.ds(0, HEAD_DIM)], load_sem.at[h, 2]),
            pltpu.make_async_copy(vt_hbm.at[:, cols], vv.at[h, :, pl.ds(HEAD_DIM, HEAD_DIM)], load_sem.at[h, 3]),
        ]
    for copy in loads:
        copy.start()

    for p, ref in enumerate((q_in, t_in)):
        for g in range(GRP):
            for h in range(heads):
                at = (g * heads + h) * HEAD_DIM
                stage[p, g, h : h + 1, :] = ref[0:1, at : at + HEAD_DIM].astype(F32)

    pl.semaphore_wait(barrier, (Z - 1) + (Y - 1) + (2 * X - 1) + jnp.where(core != zh, ZL, 0))

    row = x * 2 + core

    def x_copy(x_, p):
        return remote(stage.at[p, pl.ds(x_ * ZH, ZH)], xrecv.at[row], xs_sem.at[x_, p], xr_sem.at[row],
                      device(x_, y, z, p))

    for d in range(X):
        x_ = lax.rem(x + d, X)
        if d:
            x_copy(x_, core).start()
        x_copy(x_, other).start()
    xrecv[row] = stage[core, pl.ds(x * ZH, ZH)]
    for d in range(X):
        x_ = lax.rem(x + d, X)
        for c in ([other] if d == 0 else [core, other]):
            slot = x_ * 2 + c
            remote(stage.at[0, pl.ds(0, ZH)], xrecv.at[slot], xs_sem.at[0, 0], xr_sem.at[slot], here).wait_recv()
    for g in range(ZH):
        for h in range(heads):
            zsend[g, h] = xrecv[:, g, h, :].astype(BF16)

    def z_copy(z_):
        return remote(zsend.at[lax.div(z_, ZL)], qbuf.at[core, y, z], zs_sem.at[z_], zr_sem.at[z],
                      device(x, y, z_, core))

    order = []
    for k in range(1, Z // 2 + 1):
        order += [k] if 2 * k == Z else [k, Z - k]
    for k in reversed(order):
        z_copy(lax.rem(z + k, Z)).start()
    qbuf[core, y, z] = zsend[zh]

    def y_copy(z_, d):
        y_ = lax.rem(y + d, Y)
        return remote(qbuf.at[core, y, z_], qbuf.at[core, y, z_], ys_sem.at[d, z_], yr_sem.at[y],
                      device(x, y_, z, core))

    def own_copy(z_):
        return remote(qbuf.at[core, y, z_], qbuf.at[core, y, z_], fs_sem.at[y, z_], fr_sem.at[y], partner)

    def forward(z_):
        for d in (2, 1, 3):
            if d < Y:
                y_copy(z_, d).start()
        own_copy(z_).start()

    forward(z)

    def z_step(j, carry):
        half = lax.div(j + 1, 2)
        k = jnp.where(lax.rem(j, 2) == 1, half, Z - half)
        z_ = lax.rem(z + k, Z)
        remote(zsend.at[0], qbuf.at[core, y, z_], zs_sem.at[0], zr_sem.at[z_], here).wait_recv()
        forward(z_)
        return carry

    lax.fori_loop(1, Z, z_step, 0)

    def block_copy(y_):
        return remote(qbuf.at[core, y_], qbuf.at[core, y_], fs_sem.at[y_, 0], fr_sem.at[y_], partner)

    def take(y_):
        remote(qbuf.at[core, y_], qbuf.at[core, y_], ys_sem.at[0, 0], yr_sem.at[y_], here).wait_recv()
        block_copy(y_).start()

    def ready(y_):
        remote(qbuf.at[other, y_], qbuf.at[other, y_], fs_sem.at[0, 0], fr_sem.at[y_], here).wait_recv()

    rows = Z * B
    scale = HEAD_DIM ** -0.5

    def attend(y_):
        def one_head(h, carry):
            q = qbuf[0, y_, :, h].astype(F32).reshape(rows, HEAD_DIM).astype(BF16)
            t = qbuf[1, y_, :, h].astype(F32).reshape(rows, HEAD_DIM).astype(BF16)
            left = jnp.concatenate(
                [jnp.concatenate([q, jnp.zeros_like(q)], axis=1), jnp.concatenate([t, q], axis=1)], axis=0)
            both = lax.dot_general(left, kk[h], (((1,), (1,)), ((), ())), preferred_element_type=F32)
            scores, tangents = both[:rows] * scale, both[rows:] * scale
            top = jnp.max(scores, axis=1, keepdims=True)
            weights = jnp.exp(scores - top)
            mixed = weights * tangents
            whole = jnp.sum(weights, axis=1, keepdims=True)
            whole_t = jnp.sum(mixed, axis=1, keepdims=True)
            low = jnp.concatenate([weights.astype(BF16), mixed.astype(BF16)], axis=0)
            sums = lax.dot_general(low, vv[h], (((1,), (0,)), ((), ())), preferred_element_type=F32)
            numer = sums[:rows, :HEAD_DIM]
            numer_t = sums[:rows, HEAD_DIM:] + sums[rows:, :HEAD_DIM]
            out = numer / whole
            score = whole_t / whole
            tan = numer_t / whole - out * score
            mine[y_, :, h] = out.reshape(Z, B, HEAD_DIM).astype(BF16)
            mine[y_, :, heads + h] = tan.reshape(Z, B, HEAD_DIM).astype(BF16)
            lane = lax.broadcasted_iota(jnp.int32, (rows, 128), 1)
            stat[...] = jnp.where(lane == h, top + jnp.log(whole), jnp.where(lane == heads + h, score, stat[...]))
            return carry

        lax.fori_loop(0, heads, one_head, 0)
        mine[y_, :, 2 * heads] = pieces(stat[...], heads).reshape(Z, B, 128).astype(BF16)
        part_copy(y_).start()

    def part_copy(y_):
        return remote(mine.at[y_, pl.ds(other * ZL, ZL)], theirs.at[y_], ps_sem.at[y_], pr_sem.at[y_], partner)

    def join(y_):
        remote(theirs.at[y_], theirs.at[y_], ps_sem.at[0], pr_sem.at[y_], here).wait_recv()

        def step(i, carry):
            parts = Planes([mine.at[y_, core * ZL + i], theirs.at[y_, i]])
            outs, tans, merged = merge(parts, heads)
            for h in range(heads):
                pair[y_, i, h] = outs[h].astype(BF16)
                pair[y_, i, heads + h] = tans[h].astype(BF16)
            pair[y_, i, 2 * heads] = pieces(merged, heads).astype(BF16)
            return carry

        lax.fori_loop(0, ZL, step, 0)

    def row_copy(d):
        y_ = lax.rem(y + d, Y)
        return remote(pair.at[y_], yrecv.at[y], rs_sem.at[d], rr_sem.at[y], device(x, y_, z, core))

    turn = [d for d in (1, 3, 2) if d < Y]
    ys = [lax.rem(y + d, Y) for d in turn]

    stat[...] = jnp.zeros_like(stat)
    for copy in loads:
        copy.wait()
    ready(y)
    attend(y)
    take(ys[0])
    if len(ys) > 1:
        take(ys[1])
    for i, d in enumerate(turn):
        ready(ys[i])
        attend(ys[i])
        if i + 2 < len(ys):
            take(ys[i + 2])
        if i:
            join(ys[i - 1])
            row_copy(turn[i - 1]).start()
    join(ys[-1])
    row_copy(turn[-1]).start()
    join(y)
    for y_ in ys:
        remote(pair.at[0], yrecv.at[y_], rs_sem.at[0], rr_sem.at[y_], here).wait_recv()

    def z_target(i):
        return core * ZL + i

    def c_copy(i):
        return remote(total.at[i], zrecv.at[zl], cs_sem.at[i], cr_sem.at[zl], device(x, y, z_target(i), zh))

    def y_sum(i, carry):
        parts = Planes([pair.at[y, i]] + [yrecv.at[y_, i] for y_ in ys])
        outs, tans, merged = merge(parts, heads)
        for h in range(heads):
            total[i, h] = outs[h].astype(BF16)
            total[i, heads + h] = tans[h].astype(BF16)
        total[i, 2 * heads] = pieces(merged, heads).astype(BF16)

        @pl.when(z_target(i) != z)
        def _():
            c_copy(i).start()

        @pl.when(z_target(i) == z)
        def _():
            zrecv[zl] = total[i]

        return carry

    lax.fori_loop(0, ZL, y_sum, 0)

    def c_wait(i, carry):
        @pl.when(z_target(i) != z)
        def _():
            remote(total.at[0], zrecv.at[i], cs_sem.at[0], cr_sem.at[i], here).wait_recv()

        return carry

    lax.fori_loop(0, ZL, c_wait, 0)
    outs, tans, _ = merge(Planes([zrecv.at[i] for i in range(ZL)]), heads)
    for h in range(heads):
        final[:, 0, h, :] = outs[h]
        final[:, 1, h, :] = tans[h]

    group = x * ZH + core

    def e_copy(x_, c):
        return remote(final.at[x_ * 2 + c], orecv.at[group], es_sem.at[x_ * 2 + c], er_sem.at[group],
                      device(x_, y, z, c))

    for d in range(X):
        x_ = lax.rem(x + d, X)
        if d:
            e_copy(x_, core).start()
        e_copy(x_, other).start()
    orecv[group] = final[row]
    for d in range(X):
        x_ = lax.rem(x + d, X)
        for c in ([other] if d == 0 else [core, other]):
            slot = x_ * ZH + c
            remote(final.at[0], orecv.at[slot], es_sem.at[0], er_sem.at[slot], here).wait_recv()
    for p, ref in enumerate((o_out, t_out)):
        for g in range(GRP):
            for h in range(heads):
                at = (g * heads + h) * HEAD_DIM
                ref[0:1, at : at + HEAD_DIM] = orecv[g, p, h : h + 1, :].astype(BF16)

    for d in range(X):
        x_ = lax.rem(x + d, X)
        for c in ([other] if d == 0 else [core, other]):
            x_copy(x_, c).wait_send()
            e_copy(x_, c).wait_send()

    def sent(j, carry):
        z_ = lax.rem(z + j, Z)

        @pl.when(j > 0)
        def _():
            z_copy(z_).wait_send()

        for d in range(1, Y):
            y_copy(z_, d).wait_send()
        own_copy(z_).wait_send()
        return carry

    lax.fori_loop(0, Z, sent, 0)
    for d, y_ in zip(turn, ys):
        block_copy(y_).wait_send()
        part_copy(y_).wait_send()
        row_copy(d).wait_send()
    part_copy(y).wait_send()

    def c_sent(i, carry):
        @pl.when(z_target(i) != z)
        def _():
            c_copy(i).wait_send()

        return carry

    lax.fori_loop(0, ZL, c_sent, 0)


def per_device(queries, query_tangent, keys, key_tangent, values, value_tangent):
    count, width = keys.shape
    heads = width // HEAD_DIM
    planes = 2 * heads + 1
    pad = -(-heads // 8) * 8
    vmem, anywhere = pl.BlockSpec(memory_space=pltpu.VMEM), pl.BlockSpec(memory_space=pl.ANY)
    dma = pltpu.SemaphoreType.DMA
    return pl.pallas_call(
        functools.partial(kernel, heads),
        out_shape=(jax.ShapeDtypeStruct(queries.shape, BF16), jax.ShapeDtypeStruct(queries.shape, BF16)),
        in_specs=[vmem, vmem] + [anywhere] * 4,
        out_specs=(vmem, vmem),
        scratch_shapes=[
            pltpu.VMEM((heads, count, 2 * HEAD_DIM), BF16),
            pltpu.VMEM((heads, count, 2 * HEAD_DIM), BF16),
            pltpu.VMEM((2, GRP, pad, HEAD_DIM), F32),
            pltpu.VMEM((B, ZH, pad, HEAD_DIM), F32),
            pltpu.VMEM((ZH, heads, B, HEAD_DIM), BF16),
            pltpu.VMEM((2, Y, Z, heads, B, HEAD_DIM), BF16),
            pltpu.VMEM((Z * B, 128), F32),
            pltpu.VMEM((Y, Z, planes, B, HEAD_DIM), BF16),
            pltpu.VMEM((Y, ZL, planes, B, HEAD_DIM), BF16),
            pltpu.VMEM((Y, ZL, planes, B, HEAD_DIM), BF16),
            pltpu.VMEM((Y, ZL, planes, B, HEAD_DIM), BF16),
            pltpu.VMEM((ZL, planes, B, HEAD_DIM), BF16),
            pltpu.VMEM((ZL, planes, B, HEAD_DIM), BF16),
            pltpu.VMEM((B, 2, pad, HEAD_DIM), F32),
            pltpu.VMEM((GRP, 2, pad, HEAD_DIM), F32),
            dma((heads, 4)),
            dma((X, 2)), dma((B,)),
            dma((Z,)), dma((Z,)),
            dma((Y, Z)), dma((Y,)),
            dma((Y, Z)), dma((Y,)),
            dma((Y,)), dma((Y,)),
            dma((Y,)), dma((Y,)),
            dma((ZL,)), dma((ZL,)),
            dma((B,)), dma((GRP,)),
        ],
        compiler_params=pltpu.CompilerParams(collective_id=0, has_side_effects=True, vmem_limit_bytes=40 * 2**20),
        name="attention_tangent",
    )(queries, query_tangent, keys, key_tangent, values, value_tangent)


def solution(mesh):
    in_specs = (
        P(("grp", "seq"), None),
        P(("grp", "seq"), None),
        P("seq", "grp"),
        P("seq", "grp"),
        P("seq", "grp"),
        P("seq", "grp"),
    )
    out_specs = (P(("grp", "seq"), None), P(("grp", "seq"), None))
    return jax.shard_map(
        per_device, mesh=mesh, in_specs=in_specs, out_specs=out_specs, check_vma=False
    )
```

time: 404 us -> 86.3 us (0.21)
  waiting for transfers between devices: 161 us -> 0 us
  blocking collectives: 137 us -> 0 us
  Pallas kernels: 0 us -> 78.2 us
  starting transfers between devices: 34.7 us -> 0 us
  local copies, waits for them, and re-layouts: 39.3 us -> 7.01 us
  between operations: 14.2 us -> 0.65 us
  matrix products: 7.54 us -> 0 us
  other arithmetic: 6.58 us -> 0 us
    all_to_all x1 -> x0, blocking collectives: 137 us -> none  [sent_together(): lax.all_to_all(both, axis, split_axis=split_dim, concat_axis=concat_dim,...]
    all_gather x1 -> x0, waiting for transfers between devices: 111 us -> none  [side_by_side(): lax.all_gather(both, axis, axis=dim, tiled=True)]
    pallas_call x0 -> x1, Pallas kernels: none -> 78.2 us  [per_device(): pl.pallas_call(functools.partial(kernel, heads), out_shape=(jax.ShapeDtyp...]
    all_to_all x4 -> x0, waiting for transfers between devices: 50.5 us -> none  [the longest x2 25.2 us: several_exchanges(): lax.all_to_all(slab, axis, split_axis=0, concat_axis=0, tiled=True)]
    all_to_all x4 -> x0, starting transfers between devices: 34.7 us -> none  [the longest x2 21.4 us: several_exchanges(): lax.all_to_all(slab, axis, split_axis=0, concat_axis=0, tiled=True)]
    concatenate x1 -> x0, local copies, waits for them, and re-layouts: 15.1 us -> none  [sent_together(): both = jnp.concatenate(arrays, axis=along)]
    dot_general x6 -> x0, matrix products: 7.54 us -> none  [the longest x1 1.94 us: per_device(): jnp.einsum('qhd,khd->hqk', query3, ktan3, preferred_element_type=jnp.floa...]
    unnamed x19 -> x14, local copies, waits for them, and re-layouts: 13.6 us -> 7.01 us
  transfers between devices with their start and end apart: 5 -> 0, of which waited for: 5 -> 0; matrix products, arithmetic and copies ran while one was open for 2% -> 0% of each run, Pallas kernels for 0% -> 0%
where the time goes in v1:
time: 86.3 us; the launch traced here: 85.9 us
  Pallas kernels  78.2 us (91%)
  local copies, waits for them, and re-layouts  7.01 us (8%)
    pallas_call x1, Pallas kernels, per_device(): pl.pallas_call(functools.partial(kernel, heads), out_shape=(jax.ShapeDtyp...  78.2 us
    unnamed x14, local copies, waits for them, and re-layouts  7.01 us

profile of v1, /device:TPU:1, one launch (start us, length us, event | category | flops | bytes accessed | tf_op | source)
XLA Modules:
  0.0 85.9 jit_solution(5304078254761548724)
XLA Ops:
  0.6 0.0 copy-start
  0.6 1.1 %copy-done = bf16[512,640]{1,0:T(8,128)(2,1)S(1)} copy-done((bf16[512,640]{1,0:T(8,128)(2,1)S(1)}, bf16[512,640]{1,0:T(8,128)(2,1)}, u32[]{:S(2)}) %copy-start) | copy-done | bytes 655384
  1.7 0.0 copy-start.1
  1.7 1.1 %copy-done.1 = bf16[512,640]{1,0:T(8,128)(2,1)S(1)} copy-done((bf16[512,640]{1,0:T(8,128)(2,1)S(1)}, bf16[512,640]{1,0:T(8,128)(2,1)}, u32[]{:S(2)}) %copy-start.1) | copy-done | bytes 655384
  2.8 0.0 copy-start.2
  2.8 1.1 %copy-done.2 = bf16[512,640]{1,0:T(8,128)(2,1)S(1)} copy-done((bf16[512,640]{1,0:T(8,128)(2,1)S(1)}, bf16[512,640]{1,0:T(8,128)(2,1)}, u32[]{:S(2)}) %copy-start.2) | copy-done | bytes 655384
  3.9 0.0 copy-start.3
  3.9 1.1 %copy-done.3 = bf16[512,640]{1,0:T(8,128)(2,1)S(1)} copy-done((bf16[512,640]{1,0:T(8,128)(2,1)S(1)}, bf16[512,640]{1,0:T(8,128)(2,1)}, u32[]{:S(2)}) %copy-start.3) | copy-done | bytes 655384
  5.0 0.0 copy-start.4
  5.0 0.7 copy-done.4
  5.7 0.0 copy-start.5
  5.7 0.7 copy-done.5
  6.4 78.2 %attention_tangent.1 = (bf16[1,5120]{1,0:T(2,128)(2,1)S(1)}, bf16[1,5120]{1,0:T(2,128)(2,1)S(1)}) custom-call(bf16[1,5120]{1,0:T(2,128)(2,1)S(1)} %copy-done.4, bf16[1,5120]{1,0:T(2,128)(2,1)S(1)} %copy-done.5, bf16[512,640]{1,0:T(8,128)(2,1)S(1)} %copy-done, bf16[512,640]{1,0:T(8,128)(2,1)S(1)} %copy-done.1, bf16[512,640]{1,0:T(8,128)(2,1)S(1)} %copy-done.2, ...), custom_call_target="tpu_custom_call" | custom-call | tf_op jit(solution)/shard_map/attention_tangent/pallas_call | solution.py:378
  84.6 0.6 copy.10
  85.3 0.6 copy.11
Async XLA Ops:
  0.6 1.1 %copy-start = (bf16[512,640]{1,0:T(8,128)(2,1)S(1)}, bf16[512,640]{1,0:T(8,128)(2,1)}, u32[]{:S(2)}) copy-start(bf16[512,640]{1,0:T(8,128)(2,1)} %k_hbm.1) | copy-start | bytes 1966084
  1.7 1.1 %copy-start.1 = (bf16[512,640]{1,0:T(8,128)(2,1)S(1)}, bf16[512,640]{1,0:T(8,128)(2,1)}, u32[]{:S(2)}) copy-start(bf16[512,640]{1,0:T(8,128)(2,1)} %kt_hbm.1) | copy-start | bytes 1966084
  2.8 1.1 %copy-start.2 = (bf16[512,640]{1,0:T(8,128)(2,1)S(1)}, bf16[512,640]{1,0:T(8,128)(2,1)}, u32[]{:S(2)}) copy-start(bf16[512,640]{1,0:T(8,128)(2,1)} %v_hbm.1) | copy-start | bytes 1966084
  3.9 1.1 %copy-start.3 = (bf16[512,640]{1,0:T(8,128)(2,1)S(1)}, bf16[512,640]{1,0:T(8,128)(2,1)}, u32[]{:S(2)}) copy-start(bf16[512,640]{1,0:T(8,128)(2,1)} %vt_hbm.1) | copy-start | bytes 1966084
  5.0 0.7 copy-start.4
  5.7 0.7 copy-start.5
